TPU v7x, 32 devices: a whole 2x2x4 slice. The times are simulated.
32 devices in a mesh: section: 2 (over x), dp: 16 (over z, y, core).
Axes of the slice: x: 2, y: 2, z: 4, core: 2. Of those that a mesh axis runs over, the one named last changes fastest.
Arguments:
- activations: bfloat16 [2, 8, 768, 5376], P('section', None, 'dp'), may hold values from -6 to 6
- loss_grads: bfloat16 [8, 768, 5376], P(None, 'dp'), may hold values from -6 to 6
- adapter_in: bfloat16 [2, 5376, 64], P('section'), may hold values from -0.078125 to 0.078125
- adapter_out: bfloat16 [2, 64, 5376], P('section'), may hold values from -0.75 to 0.75
- first_moment: float32 [2, 16, 86016], P('section', 'dp'), may hold values from -0.4 to 0.4
- second_moment: float32 [2, 16, 86016], P('section', 'dp'), may hold values from 0.0001 to 0.01
- old_owner: int32 [2, 8], P('section'), may hold values from 0 to 15, as said below
- new_owner: int32 [2, 16], P('section'), may hold values from 0 to 15, each once within a row
- plan: int32 [8], replicated, may hold values from 0 to 7, each once
Outputs:
- input_grads: bfloat16 [2, 8, 768, 5376], P('section', None, 'dp')
- adam_update: float32 [2, 16, 43008], P('section', 'dp')
- first_new: float32 [2, 16, 43008], P('section', 'dp')
- second_new: float32 [2, 16, 43008], P('section', 'dp')
Inputs may be any that keep to these rules, and one draw needn't show every extreme that they name: `old_owner`: the entries of one section's row are distinct.
All inputs are finite; a program needn't handle non-finite values.
Results may differ from a plain program's by a relative error of at most 0.025.
Values may be sent and summed in bfloat16 or wider, within the bound.
A program may use at most 64 MiB of HBM per device.

v0:
```python
import jax
import jax.numpy as jnp
from jax import lax
from jax.sharding import PartitionSpec as P

beta_one = 0.9
beta_two = 0.95
adam_eps = 1e-08
adam_step = 1000.0
loss_scale = 4096.0


def passed_along(value, axis, steps):
    count = lax.axis_size(axis)
    first, last = (max(0, -steps), min(count, count - steps))
    return lax.ppermute(value, axis, [(source, source + steps) for source in range(first, last)])


def silu_slope(pre_value):
    gate_value = jax.nn.sigmoid(pre_value)
    return gate_value * (1.0 + pre_value * (1.0 - gate_value))


def per_device(
    activations,
    loss_grads,
    adapter_in,
    adapter_out,
    first_moment,
    second_moment,
    old_owner,
    new_owner,
    plan,
):
    sections = lax.axis_size("section")
    section_index = lax.axis_index("section")
    replicas = lax.axis_size("dp")
    my_index = lax.axis_index("dp")
    weight_in = adapter_in[0]
    weight_out = adapter_out[0]
    inputs_all = activations[0]
    micro_count = inputs_all.shape[0]
    tok_rows = inputs_all.shape[1]
    width = inputs_all.shape[2]
    owners_old = old_owner[0]
    owners_new = new_owner[0]
    block_len = first_moment.shape[2] // 2
    replica_ids = jnp.arange(replicas, dtype=jnp.int32)
    new_block = jnp.sum(jnp.where(owners_new == my_index, replica_ids, 0))

    def drain_turn(turn_index, state):
        previous, grad_in, grad_out, emitted = state
        received = passed_along(previous, "section", -1)
        slot = turn_index - (sections - 1 - section_index)
        is_valid = (slot >= 0) & (slot < micro_count)
        clamped = jnp.clip(slot, 0, micro_count - 1)
        micro = lax.dynamic_index_in_dim(plan, clamped, 0, keepdims=False)
        section_input = lax.dynamic_index_in_dim(inputs_all, micro, 0, keepdims=False)
        from_loss = lax.dynamic_index_in_dim(loss_grads, micro, 0, keepdims=False)
        incoming = jnp.where(section_index == sections - 1, from_loss, received)
        pre_value = jnp.dot(section_input, weight_in, preferred_element_type=jnp.float32)
        hidden = jax.nn.silu(pre_value).astype(jnp.bfloat16)
        act_grad = jnp.dot(incoming, weight_out.T, preferred_element_type=jnp.float32)
        pre_grad = (act_grad * silu_slope(pre_value)).astype(jnp.bfloat16)
        input_grad = (
            incoming.astype(jnp.float32)
            + jnp.dot(pre_grad, weight_in.T, preferred_element_type=jnp.float32)
        ).astype(jnp.bfloat16)
        valid_weight = is_valid.astype(jnp.float32)
        grad_in = grad_in + valid_weight * jnp.dot(
            section_input.T, pre_grad, preferred_element_type=jnp.float32
        )
        grad_out = grad_out + valid_weight * jnp.dot(
            hidden.T, incoming, preferred_element_type=jnp.float32
        )
        earlier = lax.dynamic_index_in_dim(emitted, clamped, 0, keepdims=False)
        written = jnp.where(is_valid, input_grad, earlier)
        emitted = lax.dynamic_update_index_in_dim(emitted, written, clamped, 0)
        return (input_grad, grad_in, grad_out, emitted)

    start_state = (
        jnp.zeros((tok_rows, width), jnp.bfloat16),
        jnp.zeros(weight_in.shape, jnp.float32),
        jnp.zeros(weight_out.shape, jnp.float32),
        jnp.zeros((micro_count, tok_rows, width), jnp.bfloat16),
    )
    last_grad, grad_in, grad_out, emitted = lax.fori_loop(
        0, micro_count + sections - 1, drain_turn, start_state
    )
    partial_value = jnp.concatenate([grad_in.reshape(-1), grad_out.reshape(-1)])
    totals = lax.psum(partial_value, "dp")
    grads = lax.dynamic_slice_in_dim(totals, new_block * block_len, block_len) / loss_scale
    old_count = owners_old.shape[0]
    piece_len = 2 * block_len // replicas
    first_pieces = first_moment[0, 0].reshape(replicas, piece_len)
    second_pieces = second_moment[0, 0].reshape(replicas, piece_len)
    first_spread = lax.all_to_all(first_pieces, "dp", split_axis=0, concat_axis=0, tiled=True)
    second_spread = lax.all_to_all(second_pieces, "dp", split_axis=0, concat_axis=0, tiled=True)
    first_held = jnp.take(first_spread, owners_old, axis=0)
    second_held = jnp.take(second_spread, owners_old, axis=0)
    my_half = my_index // old_count
    targets = owners_new.reshape(-1, 2)
    target_of_block = jnp.where(my_half == 0, targets[:, 0], targets[:, 1])
    picker = (target_of_block[None, :] == replica_ids[:, None]).astype(jnp.float32)
    first_out = jnp.dot(picker, first_held, precision=lax.Precision.HIGHEST)
    second_out = jnp.dot(picker, second_held, precision=lax.Precision.HIGHEST)
    first_got = lax.all_to_all(first_out, "dp", split_axis=0, concat_axis=0, tiled=True)
    second_got = lax.all_to_all(second_out, "dp", split_axis=0, concat_axis=0, tiled=True)
    half_start = new_block % 2 * old_count
    first_mine = lax.dynamic_slice_in_dim(first_got, half_start, old_count, 0).reshape(-1)
    second_mine = lax.dynamic_slice_in_dim(second_got, half_start, old_count, 0).reshape(-1)
    moved = (first_mine, second_mine)
    first_old, second_old = moved
    first_next = beta_one * first_old + (1.0 - beta_one) * grads
    second_next = beta_two * second_old + (1.0 - beta_two) * grads * grads
    update = (
        first_next
        / (1.0 - beta_one**adam_step)
        / (jnp.sqrt(second_next / (1.0 - beta_two**adam_step)) + adam_eps)
    )
    return (emitted[None], update[None, None], first_next[None, None], second_next[None, None])


def solution(mesh):
    placed = (
        P("section", None, "dp", None),
        P(None, "dp", None),
        P("section", None, None),
        P("section", None, None),
        P("section", "dp", None),
        P("section", "dp", None),
        P("section", None),
        P("section", None),
        P(),
    )
    return jax.shard_map(
        per_device,
        mesh=mesh,
        in_specs=placed,
        out_specs=(
            P("section", None, "dp", None),
            P("section", "dp", None),
            P("section", "dp", None),
            P("section", "dp", None),
        ),
        check_vma=False,
    )
```

profile of v0, /device:TPU:0, one launch (start us, length us, event | category | flops | bytes accessed | tf_op | source)
XLA Modules:
  0.0 360.3 jit_solution(12223333010346438085)
XLA Ops:
  7.2 7.6 %all-to-all-start.2 = ((f32[16,1,5376]{2,1,0:T(1,128)}), f32[16,1,5376]{2,1,0:T(1,128)S(1)}, u32[]{:S(2)}, u32[]{:S(2)}) async-start(f32[16,1,5376]{2,1,0:T(1,128)} %bitcast.84), calls=%async_computation.2 | async-start | bytes 688128 | tf_op jit(solution)/shard_map/all_to_all | solution.py:98
  17.8 8.3 %all-to-all-done.2 = f32[16,1,5376]{2,1,0:T(1,128)S(1)} async-done(((f32[16,1,5376]{2,1,0:T(1,128)}), f32[16,1,5376]{2,1,0:T(1,128)S(1)}, u32[]{:S(2)}, u32[]{:S(2)}) %all-to-all-start.2) | async-done | bytes 344096 | tf_op jit(solution)/shard_map/all_to_all | solution.py:98
  26.1 4.2 %all-to-all-start = ((f32[16,1,5376]{2,1,0:T(1,128)}), f32[16,1,5376]{2,1,0:T(1,128)}, u32[]{:S(2)}, u32[]{:S(2)}) async-start(f32[16,1,5376]{2,1,0:T(1,128)} %bitcast.5), calls=%async_computation | async-start | bytes 688128 | tf_op jit(solution)/shard_map/all_to_all | solution.py:97
  30.3 2.3 broadcast_in_dim.52
  32.6 192.7 %while.22 = (s32[]{:T(128)}, bf16[48,5376]{1,0:T(8,128)(2,1)}, f32[5376,64]{0,1:T(8,128)S(1)}, f32[64,5376]{1,0:T(8,128)}, bf16[8,48,5376]{2,1,0:T(8,128)(2,1)},...) while((s32[]{:T(128)}, bf16[48,5376]{1,0:T(8,128)(2,1)}, ...), condition=%wide.region_1.2_spmd.clone, body=%wide.region_0.1_spmd.clone.sunk | while | flops 168806416 | bytes 28440968 | solution.py:87
  39.9 9.6 %collective-permute-done = bf16[48,5376]{1,0:T(8,128)(2,1)} collective-permute-done((bf16[48,5376]{1,0:T(8,128)(2,1)}, bf16[48,5376]{1,0:T(8,128)(2,1)}, u32[]{:S(2)}, u32[]{:S(2)}) %collective-permute-start) | collective-permute-done | bytes 516128 | tf_op jit(solution)/shard_map/while/body/eval_jaxpr/ppermute | solution.py:16
  52.7 1.7 fusion.54
  56.1 1.9 broadcast_select_fusion.2
  64.5 8.7 %collective-permute-done = bf16[48,5376]{1,0:T(8,128)(2,1)} collective-permute-done((bf16[48,5376]{1,0:T(8,128)(2,1)}, bf16[48,5376]{1,0:T(8,128)(2,1)}, u32[]{:S(2)}, u32[]{:S(2)}) %collective-permute-start) | collective-permute-done | bytes 516128 | tf_op jit(solution)/shard_map/while/body/eval_jaxpr/ppermute | solution.py:16
  79.8 1.9 broadcast_select_fusion.2
  88.1 7.9 %collective-permute-done = bf16[48,5376]{1,0:T(8,128)(2,1)} collective-permute-done((bf16[48,5376]{1,0:T(8,128)(2,1)}, bf16[48,5376]{1,0:T(8,128)(2,1)}, u32[]{:S(2)}, u32[]{:S(2)}) %collective-permute-start) | collective-permute-done | bytes 516128 | tf_op jit(solution)/shard_map/while/body/eval_jaxpr/ppermute | solution.py:16
  102.6 1.9 broadcast_select_fusion.2
  111.0 7.0 %collective-permute-done = bf16[48,5376]{1,0:T(8,128)(2,1)} collective-permute-done((bf16[48,5376]{1,0:T(8,128)(2,1)}, bf16[48,5376]{1,0:T(8,128)(2,1)}, u32[]{:S(2)}, u32[]{:S(2)}) %collective-permute-start) | collective-permute-done | bytes 516128 | tf_op jit(solution)/shard_map/while/body/eval_jaxpr/ppermute | solution.py:16
  124.6 1.9 broadcast_select_fusion.2
  132.9 6.2 %collective-permute-done = bf16[48,5376]{1,0:T(8,128)(2,1)} collective-permute-done((bf16[48,5376]{1,0:T(8,128)(2,1)}, bf16[48,5376]{1,0:T(8,128)(2,1)}, u32[]{:S(2)}, u32[]{:S(2)}) %collective-permute-start) | collective-permute-done | bytes 516128 | tf_op jit(solution)/shard_map/while/body/eval_jaxpr/ppermute | solution.py:16
  145.7 1.9 broadcast_select_fusion.2
  154.1 5.3 %collective-permute-done = bf16[48,5376]{1,0:T(8,128)(2,1)} collective-permute-done((bf16[48,5376]{1,0:T(8,128)(2,1)}, bf16[48,5376]{1,0:T(8,128)(2,1)}, u32[]{:S(2)}, u32[]{:S(2)}) %collective-permute-start) | collective-permute-done | bytes 516128 | tf_op jit(solution)/shard_map/while/body/eval_jaxpr/ppermute | solution.py:16
  166.0 1.9 broadcast_select_fusion.2
  174.4 4.8 %collective-permute-done = bf16[48,5376]{1,0:T(8,128)(2,1)} collective-permute-done((bf16[48,5376]{1,0:T(8,128)(2,1)}, bf16[48,5376]{1,0:T(8,128)(2,1)}, u32[]{:S(2)}, u32[]{:S(2)}) %collective-permute-start) | collective-permute-done | bytes 516128 | tf_op jit(solution)/shard_map/while/body/eval_jaxpr/ppermute | solution.py:16
  182.3 1.7 fusion.54
  185.8 1.9 broadcast_select_fusion.2
  194.1 4.8 %collective-permute-done = bf16[48,5376]{1,0:T(8,128)(2,1)} collective-permute-done((bf16[48,5376]{1,0:T(8,128)(2,1)}, bf16[48,5376]{1,0:T(8,128)(2,1)}, u32[]{:S(2)}, u32[]{:S(2)}) %collective-permute-start) | collective-permute-done | bytes 516128 | tf_op jit(solution)/shard_map/while/body/eval_jaxpr/ppermute | solution.py:16
  205.5 1.9 broadcast_select_fusion.2
  213.9 4.8 %collective-permute-done = bf16[48,5376]{1,0:T(8,128)(2,1)} collective-permute-done((bf16[48,5376]{1,0:T(8,128)(2,1)}, bf16[48,5376]{1,0:T(8,128)(2,1)}, u32[]{:S(2)}, u32[]{:S(2)}) %collective-permute-start) | collective-permute-done | bytes 516128 | tf_op jit(solution)/shard_map/while/body/eval_jaxpr/ppermute | solution.py:16
  226.7 2.1 copy.18
  228.8 2.9 reshape.52
  234.0 5.3 %all-to-all-start.3 = ((f32[16,1,5376]{2,1,0:T(1,128)}), f32[16,1,5376]{2,1,0:T(1,128)S(1)}, u32[]{:S(2)}, u32[]{:S(2)}) async-start(f32[16,1,5376]{2,1,0:T(1,128)} %copy.19), calls=%async_computation.3 | async-start | bytes 688128 | tf_op jit(solution)/shard_map/all_to_all | solution.py:108
  239.3 1.8 pad_maximum_fusion
  247.4 3.2 all-to-all-done.3
  250.6 3.5 all-to-all-start.1
  254.3 15.2 %all-to-all-done.1 = f32[16,1,5376]{2,1,0:T(1,128)S(1)} async-done(((f32[16,1,5376]{2,1,0:T(1,128)}), f32[16,1,5376]{2,1,0:T(1,128)S(1)}, u32[]{:S(2)}, u32[]{:S(2)}) %all-to-all-start.1) | async-done | bytes 344096 | tf_op jit(solution)/shard_map/all_to_all | solution.py:107
  269.7 82.0 %all-reduce.2.cloned.1.call-done = f32[688128]{0:T(1024)} async-done(((f32[688128]{0:T(1024)}), f32[688128]{0:T(1024)}) %all-reduce.2.cloned.1.call-update) | async-done | bytes 2752528 | tf_op jit(solution)/shard_map/psum | solution.py:91
  (157 shorter events, 108.5 us)
Async XLA Ops:
  7.2 9.9 %copy-start.8 = (s32[1,16]{1,0:T(1,128)S(1)}, s32[1,16]{1,0:T(1,128)}, u32[]{:S(2)}) copy-start(s32[1,16]{1,0:T(1,128)} %param.20) | copy-start | bytes 196
  7.2 10.6 %copy-start.7 = (s32[1,8]{1,0:T(1,128)S(1)}, s32[1,8]{1,0:T(1,128)}, u32[]{:S(2)}) copy-start(s32[1,8]{1,0:T(1,128)} %param.19) | copy-start | bytes 100
  7.2 18.9 %all-to-all-start.2 = ((f32[16,1,5376]{2,1,0:T(1,128)}), f32[16,1,5376]{2,1,0:T(1,128)S(1)}, u32[]{:S(2)}, u32[]{:S(2)}) async-start(f32[16,1,5376]{2,1,0:T(1,128)} %bitcast.84), calls=%async_computation.2 | async-start | bytes 688128 | tf_op jit(solution)/shard_map/all_to_all | solution.py:98
  26.1 4.2 %copy-start.4 = (f32[16,1,5376]{2,1,0:T(1,128)}, f32[16,1,5376]{2,1,0:T(1,128)S(1)}, u32[]{:S(2)}) copy-start(f32[16,1,5376]{2,1,0:T(1,128)S(1)} %all-to-all-done.2) | copy-start | bytes 1032196
  26.1 207.9 %all-to-all-start = ((f32[16,1,5376]{2,1,0:T(1,128)}), f32[16,1,5376]{2,1,0:T(1,128)}, u32[]{:S(2)}, u32[]{:S(2)}) async-start(f32[16,1,5376]{2,1,0:T(1,128)} %bitcast.5), calls=%async_computation | async-start | bytes 688128 | tf_op jit(solution)/shard_map/all_to_all | solution.py:97
  30.3 2.3 copy-start.2
  30.3 2.3 copy-start.6
  33.4 16.1 %collective-permute-start = (bf16[48,5376]{1,0:T(8,128)(2,1)}, bf16[48,5376]{1,0:T(8,128)(2,1)}, u32[]{:S(2)}, u32[]{:S(2)}) collective-permute-start(bf16[48,5376]{1,0:T(8,128)(2,1)} %broadcast_select_fusion.2), channel_id=1, source_target_pairs={{16,0},{17,1},{18,2},{19,3},{20,4},{21,5},{22,6},{23,7},{24,8},{25... | collective-permute-start | bytes 1548296 | tf_op jit(solution)/shard_map/while/body/eval_jaxpr/ppermute | solution.py:16
  52.7 1.8 copy-start
  55.0 1.1 copy-start.1
  58.0 15.2 %collective-permute-start = (bf16[48,5376]{1,0:T(8,128)(2,1)}, bf16[48,5376]{1,0:T(8,128)(2,1)}, u32[]{:S(2)}, u32[]{:S(2)}) collective-permute-start(bf16[48,5376]{1,0:T(8,128)(2,1)} %broadcast_select_fusion.2), channel_id=1, source_target_pairs={{16,0},{17,1},{18,2},{19,3},{20,4},{21,5},{22,6},{23,7},{24,8},{25... | collective-permute-start | bytes 1548296 | tf_op jit(solution)/shard_map/while/body/eval_jaxpr/ppermute | solution.py:16
  76.4 1.8 copy-start
  78.7 1.1 copy-start.1
  81.7 14.4 %collective-permute-start = (bf16[48,5376]{1,0:T(8,128)(2,1)}, bf16[48,5376]{1,0:T(8,128)(2,1)}, u32[]{:S(2)}, u32[]{:S(2)}) collective-permute-start(bf16[48,5376]{1,0:T(8,128)(2,1)} %broadcast_select_fusion.2), channel_id=1, source_target_pairs={{16,0},{17,1},{18,2},{19,3},{20,4},{21,5},{22,6},{23,7},{24,8},{25... | collective-permute-start | bytes 1548296 | tf_op jit(solution)/shard_map/while/body/eval_jaxpr/ppermute | solution.py:16
  99.2 1.7 copy-start
  104.5 13.5 %collective-permute-start = (bf16[48,5376]{1,0:T(8,128)(2,1)}, bf16[48,5376]{1,0:T(8,128)(2,1)}, u32[]{:S(2)}, u32[]{:S(2)}) collective-permute-start(bf16[48,5376]{1,0:T(8,128)(2,1)} %broadcast_select_fusion.2), channel_id=1, source_target_pairs={{16,0},{17,1},{18,2},{19,3},{20,4},{21,5},{22,6},{23,7},{24,8},{25... | collective-permute-start | bytes 1548296 | tf_op jit(solution)/shard_map/while/body/eval_jaxpr/ppermute | solution.py:16
  121.2 1.7 copy-start
  126.4 12.7 %collective-permute-start = (bf16[48,5376]{1,0:T(8,128)(2,1)}, bf16[48,5376]{1,0:T(8,128)(2,1)}, u32[]{:S(2)}, u32[]{:S(2)}) collective-permute-start(bf16[48,5376]{1,0:T(8,128)(2,1)} %broadcast_select_fusion.2), channel_id=1, source_target_pairs={{16,0},{17,1},{18,2},{19,3},{20,4},{21,5},{22,6},{23,7},{24,8},{25... | collective-permute-start | bytes 1548296 | tf_op jit(solution)/shard_map/while/body/eval_jaxpr/ppermute | solution.py:16
  142.3 1.8 copy-start
  147.6 11.8 %collective-permute-start = (bf16[48,5376]{1,0:T(8,128)(2,1)}, bf16[48,5376]{1,0:T(8,128)(2,1)}, u32[]{:S(2)}, u32[]{:S(2)}) collective-permute-start(bf16[48,5376]{1,0:T(8,128)(2,1)} %broadcast_select_fusion.2), channel_id=1, source_target_pairs={{16,0},{17,1},{18,2},{19,3},{20,4},{21,5},{22,6},{23,7},{24,8},{25... | collective-permute-start | bytes 1548296 | tf_op jit(solution)/shard_map/while/body/eval_jaxpr/ppermute | solution.py:16
  162.6 1.8 copy-start
  167.9 11.3 %collective-permute-start = (bf16[48,5376]{1,0:T(8,128)(2,1)}, bf16[48,5376]{1,0:T(8,128)(2,1)}, u32[]{:S(2)}, u32[]{:S(2)}) collective-permute-start(bf16[48,5376]{1,0:T(8,128)(2,1)} %broadcast_select_fusion.2), channel_id=1, source_target_pairs={{16,0},{17,1},{18,2},{19,3},{20,4},{21,5},{22,6},{23,7},{24,8},{25... | collective-permute-start | bytes 1548296 | tf_op jit(solution)/shard_map/while/body/eval_jaxpr/ppermute | solution.py:16
  182.3 1.8 copy-start
  187.6 11.3 %collective-permute-start = (bf16[48,5376]{1,0:T(8,128)(2,1)}, bf16[48,5376]{1,0:T(8,128)(2,1)}, u32[]{:S(2)}, u32[]{:S(2)}) collective-permute-start(bf16[48,5376]{1,0:T(8,128)(2,1)} %broadcast_select_fusion.2), channel_id=1, source_target_pairs={{16,0},{17,1},{18,2},{19,3},{20,4},{21,5},{22,6},{23,7},{24,8},{25... | collective-permute-start | bytes 1548296 | tf_op jit(solution)/shard_map/while/body/eval_jaxpr/ppermute | solution.py:16
  202.1 1.8 copy-start
  207.4 11.3 %collective-permute-start = (bf16[48,5376]{1,0:T(8,128)(2,1)}, bf16[48,5376]{1,0:T(8,128)(2,1)}, u32[]{:S(2)}, u32[]{:S(2)}) collective-permute-start(bf16[48,5376]{1,0:T(8,128)(2,1)} %broadcast_select_fusion.2), channel_id=1, source_target_pairs={{16,0},{17,1},{18,2},{19,3},{20,4},{21,5},{22,6},{23,7},{24,8},{25... | collective-permute-start | bytes 1548296 | tf_op jit(solution)/shard_map/while/body/eval_jaxpr/ppermute | solution.py:16
  221.8 1.8 copy-start
  228.8 3.1 copy-start.5
  232.5 6.8 %copy-start.3 = (f32[344064]{0:T(1024)S(1)}, f32[344064]{0:T(1024)}, u32[]{:S(2)}) copy-start(f32[344064]{0:T(1024)} %reshape.52) | copy-start | bytes 4128772
  234.0 16.6 %all-to-all-start.3 = ((f32[16,1,5376]{2,1,0:T(1,128)}), f32[16,1,5376]{2,1,0:T(1,128)S(1)}, u32[]{:S(2)}, u32[]{:S(2)}) async-start(f32[16,1,5376]{2,1,0:T(1,128)} %copy.19), calls=%async_computation.3 | async-start | bytes 688128 | tf_op jit(solution)/shard_map/all_to_all | solution.py:108
  239.3 112.5 %all-reduce.2.cloned.1.call-start = ((), (), s32[]{:S(2)}) async-start(), calls=%async_computation.4 | async-start | bytes 5505024 | tf_op jit(solution)/shard_map/psum | solution.py:91
  250.6 18.9 %all-to-all-start.1 = ((f32[16,1,5376]{2,1,0:T(1,128)}), f32[16,1,5376]{2,1,0:T(1,128)S(1)}, u32[]{:S(2)}, u32[]{:S(2)}) async-start(f32[16,1,5376]{2,1,0:T(1,128)} %copy.17), calls=%async_computation.1 | async-start | bytes 688128 | tf_op jit(solution)/shard_map/all_to_all | solution.py:107
  (7 other events, 7.7 us)
Sparse Core Ops, SparseCore 0:
  243.7 108.0 all-reduce.1
where the time goes:
time: 363 us; the launch traced here: 360 us
  waiting for transfers between devices  168 us (46%)
  matrix products  51.1 us (14%)
  local copies, waits for them, and re-layouts  40.9 us (11%)
  other arithmetic  32.4 us (9%)
  starting transfers between devices  32.1 us (9%)
  loops' own time  19.1 us (5%)
  between operations  16.9 us (5%)
    psum x1, waiting for transfers between devices, per_device(): totals = lax.psum(partial_value, 'dp')  82 us
    ppermute x9, waiting for transfers between devices, passed_along(): lax.ppermute(value, axis, [(source, source + steps) for source in range(f...  59.2 us
    another operation x1, loops' own time, per_device(): lax.fori_loop(0, micro_count + sections - 1, drain_turn, start_state)  19.1 us
    while x9, other arithmetic  15.8 us
    dot_general x9, matrix products, drain_turn(): jnp.dot(section_input.T, pre_grad, preferred_element_type=jnp.float32)  15.7 us
    all_to_all x1, waiting for transfers between devices, per_device(): lax.all_to_all(first_out, 'dp', split_axis=0, concat_axis=0, tiled=True)  15.2 us
    dot_general x9, matrix products, drain_turn(): jnp.dot(pre_grad, weight_in.T, preferred_element_type=jnp.float32)  14.3 us
    dot_general x9, matrix products, drain_turn(): jnp.dot(section_input, weight_in, preferred_element_type=jnp.float32)  12.6 us
  transfers between devices with their start and end apart: 14, of which 13 were waited for; matrix products, arithmetic and copies ran while one was open for 31% of the time, Pallas kernels for 0%

commit v1 on v0

--- a/solution.py
+++ b/solution.py
@@ -88,7 +88,9 @@
         0, micro_count + sections - 1, drain_turn, start_state
     )
     partial_value = jnp.concatenate([grad_in.reshape(-1), grad_out.reshape(-1)])
-    totals = lax.psum(partial_value, "dp")
+    totals = partial_value
+    for hop in (1, 2, 4, 8):
+        totals = totals + lax.ppermute(totals, "dp", [(dev, dev ^ hop) for dev in range(16)])
     grads = lax.dynamic_slice_in_dim(totals, new_block * block_len, block_len) / loss_scale
     old_count = owners_old.shape[0]
     piece_len = 2 * block_len // replicas

time: 363 us -> 503 us (1.39)
  waiting for transfers between devices: 168 us -> 316 us
  between operations: 16.9 us -> 3.47 us
    ppermute x0 -> x4, waiting for transfers between devices: none -> 126 us  [per_device(): lax.ppermute(totals, 'dp', [(dev, dev ^ hop) for dev in range(16)])]
    all_to_all x1, waiting for transfers between devices: 0.01 us -> 115 us  [per_device(): lax.all_to_all(first_pieces, 'dp', split_axis=0, concat_axis=0, tiled=True)]
    psum x1 -> x0, waiting for transfers between devices: 82 us -> none  [per_device(): totals = lax.psum(partial_value, 'dp')]
    all_to_all x1, waiting for transfers between devices: 8.27 us -> 0.01 us  [per_device(): lax.all_to_all(second_pieces, 'dp', split_axis=0, concat_axis=0, tiled=True)]
    add x0 -> x3, other arithmetic: none -> 5.92 us  [per_device(): totals + lax.ppermute(totals, 'dp', [(dev, dev ^ hop) for dev in range(16)])]
  transfers between devices with their start and end apart: 14 -> 17, of which waited for: 13 -> 15; matrix products, arithmetic and copies ran while one was open for 31% -> 8% of each run, Pallas kernels for 0% -> 0%
where the time goes in v1:
time: 503 us; the launch traced here: 500 us
  waiting for transfers between devices  316 us (63%)
  matrix products  51.1 us (10%)
  local copies, waits for them, and re-layouts  40.9 us (8%)
  other arithmetic  36.6 us (7%)
  starting transfers between devices  32.1 us (6%)
  loops' own time  19.4 us (4%)
    ppermute x4, waiting for transfers between devices, per_device(): lax.ppermute(totals, 'dp', [(dev, dev ^ hop) for dev in range(16)])  126 us
    all_to_all x1, waiting for transfers between devices, per_device(): lax.all_to_all(first_pieces, 'dp', split_axis=0, concat_axis=0, tiled=True)  115 us
    ppermute x9, waiting for transfers between devices, passed_along(): lax.ppermute(value, axis, [(source, source + steps) for source in range(f...  58.6 us
    another operation x1, loops' own time, per_device(): lax.fori_loop(0, micro_count + sections - 1, drain_turn, start_state)  19.4 us
    while x9, other arithmetic  15.7 us
    dot_general x9, matrix products, drain_turn(): jnp.dot(section_input.T, pre_grad, preferred_element_type=jnp.float32)  15.7 us
    dot_general x9, matrix products, drain_turn(): jnp.dot(pre_grad, weight_in.T, preferred_element_type=jnp.float32)  14.3 us
    dot_general x9, matrix products, drain_turn(): jnp.dot(section_input, weight_in, preferred_element_type=jnp.float32)  12.6 us
  transfers between devices with their start and end apart: 17, of which 15 were waited for; matrix products, arithmetic and copies ran while one was open for 8% of the time, Pallas kernels for 0%

profile of v1, /device:TPU:0, one launch (start us, length us, event | category | flops | bytes accessed | tf_op | source)
XLA Modules:
  0.0 499.9 jit_solution(18273292959889319755)
XLA Ops:
  2.4 2.3 broadcast_in_dim.52
  4.7 192.6 %while.22 = (s32[]{:T(128)}, bf16[48,5376]{1,0:T(8,128)(2,1)}, f32[5376,64]{0,1:T(8,128)S(1)}, f32[64,5376]{1,0:T(8,128)}, bf16[8,48,5376]{2,1,0:T(8,128)(2,1)},...) while((s32[]{:T(128)}, bf16[48,5376]{1,0:T(8,128)(2,1)}, ...), condition=%wide.region_1.2_spmd.clone, body=%wide.region_0.1_spmd.clone.sunk | while | flops 168806416 | bytes 28440968 | solution.py:87
  12.1 9.8 %collective-permute-done = bf16[48,5376]{1,0:T(8,128)(2,1)} collective-permute-done((bf16[48,5376]{1,0:T(8,128)(2,1)}, bf16[48,5376]{1,0:T(8,128)(2,1)}, u32[]{:S(2)}, u32[]{:S(2)}) %collective-permute-start) | collective-permute-done | bytes 516128 | tf_op jit(solution)/shard_map/while/body/eval_jaxpr/ppermute | solution.py:16
  28.5 1.9 broadcast_select_fusion.2
  36.9 8.6 %collective-permute-done = bf16[48,5376]{1,0:T(8,128)(2,1)} collective-permute-done((bf16[48,5376]{1,0:T(8,128)(2,1)}, bf16[48,5376]{1,0:T(8,128)(2,1)}, u32[]{:S(2)}, u32[]{:S(2)}) %collective-permute-start) | collective-permute-done | bytes 516128 | tf_op jit(solution)/shard_map/while/body/eval_jaxpr/ppermute | solution.py:16
  52.1 1.9 broadcast_select_fusion.2
  60.5 7.8 %collective-permute-done = bf16[48,5376]{1,0:T(8,128)(2,1)} collective-permute-done((bf16[48,5376]{1,0:T(8,128)(2,1)}, bf16[48,5376]{1,0:T(8,128)(2,1)}, u32[]{:S(2)}, u32[]{:S(2)}) %collective-permute-start) | collective-permute-done | bytes 516128 | tf_op jit(solution)/shard_map/while/body/eval_jaxpr/ppermute | solution.py:16
  74.9 1.9 broadcast_select_fusion.2
  83.3 6.9 %collective-permute-done = bf16[48,5376]{1,0:T(8,128)(2,1)} collective-permute-done((bf16[48,5376]{1,0:T(8,128)(2,1)}, bf16[48,5376]{1,0:T(8,128)(2,1)}, u32[]{:S(2)}, u32[]{:S(2)}) %collective-permute-start) | collective-permute-done | bytes 516128 | tf_op jit(solution)/shard_map/while/body/eval_jaxpr/ppermute | solution.py:16
  96.8 1.9 broadcast_select_fusion.2
  105.2 6.0 %collective-permute-done = bf16[48,5376]{1,0:T(8,128)(2,1)} collective-permute-done((bf16[48,5376]{1,0:T(8,128)(2,1)}, bf16[48,5376]{1,0:T(8,128)(2,1)}, u32[]{:S(2)}, u32[]{:S(2)}) %collective-permute-start) | collective-permute-done | bytes 516128 | tf_op jit(solution)/shard_map/while/body/eval_jaxpr/ppermute | solution.py:16
  117.8 1.9 broadcast_select_fusion.2
  126.2 5.2 %collective-permute-done = bf16[48,5376]{1,0:T(8,128)(2,1)} collective-permute-done((bf16[48,5376]{1,0:T(8,128)(2,1)}, bf16[48,5376]{1,0:T(8,128)(2,1)}, u32[]{:S(2)}, u32[]{:S(2)}) %collective-permute-start) | collective-permute-done | bytes 516128 | tf_op jit(solution)/shard_map/while/body/eval_jaxpr/ppermute | solution.py:16
  146.4 4.7 collective-permute-done
  157.8 1.9 broadcast_select_fusion.2
  166.2 4.8 collective-permute-done
  177.5 1.9 broadcast_select_fusion.2
  185.9 4.7 collective-permute-done
  197.3 2.1 copy.18
  199.4 2.0 reshape.52
  204.5 5.3 %collective-permute-done.1 = f32[688128]{0:T(1024)S(1)} collective-permute-done((f32[688128]{0:T(1024)}, f32[688128]{0:T(1024)S(1)}, u32[]{:S(2)}, u32[]{:S(2)}) %collective-permute-start.1) | collective-permute-done | bytes 2752544 | tf_op jit(solution)/shard_map/ppermute | solution.py:93
  209.8 2.1 add.125
  212.6 61.0 %collective-permute-done.2 = f32[688128]{0:T(1024)S(1)} collective-permute-done((f32[688128]{0:T(1024)S(1)}, f32[688128]{0:T(1024)S(1)}, u32[]{:S(2)}, u32[]{:S(2)}) %collective-permute-start.2) | collective-permute-done | bytes 2752544 | tf_op jit(solution)/shard_map/ppermute | solution.py:93
  274.7 4.8 all-to-all-start.2
  279.6 59.5 %collective-permute-done.3 = f32[688128]{0:T(1024)} collective-permute-done((f32[688128]{0:T(1024)S(1)}, f32[688128]{0:T(1024)}, u32[]{:S(2)}, u32[]{:S(2)}) %collective-permute-start.3) | collective-permute-done | bytes 2752544 | tf_op jit(solution)/shard_map/ppermute | solution.py:93
  339.1 3.6 add.127
  342.8 5.4 %all-to-all-start = ((f32[16,1,5376]{2,1,0:T(1,128)}), f32[16,1,5376]{2,1,0:T(1,128)S(1)}, u32[]{:S(2)}, u32[]{:S(2)}) async-start(f32[16,1,5376]{2,1,0:T(1,128)} %bitcast.5), calls=%async_computation | async-start | bytes 688128 | tf_op jit(solution)/shard_map/all_to_all | solution.py:99
  351.9 114.8 %all-to-all-done = f32[16,1,5376]{2,1,0:T(1,128)S(1)} async-done(((f32[16,1,5376]{2,1,0:T(1,128)}), f32[16,1,5376]{2,1,0:T(1,128)S(1)}, u32[]{:S(2)}, u32[]{:S(2)}) %all-to-all-start) | async-done | bytes 344096 | tf_op jit(solution)/shard_map/all_to_all | solution.py:99
  466.7 5.0 %all-to-all-start.3 = ((f32[16,1,5376]{2,1,0:T(1,128)}), f32[16,1,5376]{2,1,0:T(1,128)S(1)}, u32[]{:S(2)}, u32[]{:S(2)}) async-start(f32[16,1,5376]{2,1,0:T(1,128)} %copy.19), calls=%async_computation.3 | async-start | bytes 688128 | tf_op jit(solution)/shard_map/all_to_all | solution.py:110
  477.0 6.0 %all-to-all-done.3 = f32[16,1,5376]{2,1,0:T(1,128)S(1)} async-done(((f32[16,1,5376]{2,1,0:T(1,128)}), f32[16,1,5376]{2,1,0:T(1,128)S(1)}, u32[]{:S(2)}, u32[]{:S(2)}) %all-to-all-start.3) | async-done | bytes 344096 | tf_op jit(solution)/shard_map/all_to_all | solution.py:110
  483.0 3.5 all-to-all-start.1
  486.8 11.1 %all-to-all-done.1 = f32[16,1,5376]{2,1,0:T(1,128)S(1)} async-done(((f32[16,1,5376]{2,1,0:T(1,128)}), f32[16,1,5376]{2,1,0:T(1,128)S(1)}, u32[]{:S(2)}, u32[]{:S(2)}) %all-to-all-start.1) | async-done | bytes 344096 | tf_op jit(solution)/shard_map/all_to_all | solution.py:109
  (162 shorter events, 116.8 us)
Async XLA Ops:
  2.4 2.3 copy-start.3
  2.4 2.3 copy-start.4
  5.5 16.3 %collective-permute-start = (bf16[48,5376]{1,0:T(8,128)(2,1)}, bf16[48,5376]{1,0:T(8,128)(2,1)}, u32[]{:S(2)}, u32[]{:S(2)}) collective-permute-start(bf16[48,5376]{1,0:T(8,128)(2,1)} %broadcast_select_fusion.2), channel_id=1, source_target_pairs={{16,0},{17,1},{18,2},{19,3},{20,4},{21,5},{22,6},{23,7},{24,8},{25... | collective-permute-start | bytes 1548296 | tf_op jit(solution)/shard_map/while/body/eval_jaxpr/ppermute | solution.py:16
  25.0 1.8 copy-start
  30.3 15.2 %collective-permute-start = (bf16[48,5376]{1,0:T(8,128)(2,1)}, bf16[48,5376]{1,0:T(8,128)(2,1)}, u32[]{:S(2)}, u32[]{:S(2)}) collective-permute-start(bf16[48,5376]{1,0:T(8,128)(2,1)} %broadcast_select_fusion.2), channel_id=1, source_target_pairs={{16,0},{17,1},{18,2},{19,3},{20,4},{21,5},{22,6},{23,7},{24,8},{25... | collective-permute-start | bytes 1548296 | tf_op jit(solution)/shard_map/while/body/eval_jaxpr/ppermute | solution.py:16
  48.7 1.8 copy-start
  54.0 14.3 %collective-permute-start = (bf16[48,5376]{1,0:T(8,128)(2,1)}, bf16[48,5376]{1,0:T(8,128)(2,1)}, u32[]{:S(2)}, u32[]{:S(2)}) collective-permute-start(bf16[48,5376]{1,0:T(8,128)(2,1)} %broadcast_select_fusion.2), channel_id=1, source_target_pairs={{16,0},{17,1},{18,2},{19,3},{20,4},{21,5},{22,6},{23,7},{24,8},{25... | collective-permute-start | bytes 1548296 | tf_op jit(solution)/shard_map/while/body/eval_jaxpr/ppermute | solution.py:16
  71.4 1.8 copy-start
  76.7 13.4 %collective-permute-start = (bf16[48,5376]{1,0:T(8,128)(2,1)}, bf16[48,5376]{1,0:T(8,128)(2,1)}, u32[]{:S(2)}, u32[]{:S(2)}) collective-permute-start(bf16[48,5376]{1,0:T(8,128)(2,1)} %broadcast_select_fusion.2), channel_id=1, source_target_pairs={{16,0},{17,1},{18,2},{19,3},{20,4},{21,5},{22,6},{23,7},{24,8},{25... | collective-permute-start | bytes 1548296 | tf_op jit(solution)/shard_map/while/body/eval_jaxpr/ppermute | solution.py:16
  93.3 1.8 copy-start
  95.7 1.1 copy-start.1
  98.6 12.6 %collective-permute-start = (bf16[48,5376]{1,0:T(8,128)(2,1)}, bf16[48,5376]{1,0:T(8,128)(2,1)}, u32[]{:S(2)}, u32[]{:S(2)}) collective-permute-start(bf16[48,5376]{1,0:T(8,128)(2,1)} %broadcast_select_fusion.2), channel_id=1, source_target_pairs={{16,0},{17,1},{18,2},{19,3},{20,4},{21,5},{22,6},{23,7},{24,8},{25... | collective-permute-start | bytes 1548296 | tf_op jit(solution)/shard_map/while/body/eval_jaxpr/ppermute | solution.py:16
  114.4 1.8 copy-start
  119.7 11.7 %collective-permute-start = (bf16[48,5376]{1,0:T(8,128)(2,1)}, bf16[48,5376]{1,0:T(8,128)(2,1)}, u32[]{:S(2)}, u32[]{:S(2)}) collective-permute-start(bf16[48,5376]{1,0:T(8,128)(2,1)} %broadcast_select_fusion.2), channel_id=1, source_target_pairs={{16,0},{17,1},{18,2},{19,3},{20,4},{21,5},{22,6},{23,7},{24,8},{25... | collective-permute-start | bytes 1548296 | tf_op jit(solution)/shard_map/while/body/eval_jaxpr/ppermute | solution.py:16
  134.6 1.8 copy-start
  139.9 11.3 %collective-permute-start = (bf16[48,5376]{1,0:T(8,128)(2,1)}, bf16[48,5376]{1,0:T(8,128)(2,1)}, u32[]{:S(2)}, u32[]{:S(2)}) collective-permute-start(bf16[48,5376]{1,0:T(8,128)(2,1)} %broadcast_select_fusion.2), channel_id=1, source_target_pairs={{16,0},{17,1},{18,2},{19,3},{20,4},{21,5},{22,6},{23,7},{24,8},{25... | collective-permute-start | bytes 1548296 | tf_op jit(solution)/shard_map/while/body/eval_jaxpr/ppermute | solution.py:16
  154.3 1.8 copy-start
  159.6 11.3 %collective-permute-start = (bf16[48,5376]{1,0:T(8,128)(2,1)}, bf16[48,5376]{1,0:T(8,128)(2,1)}, u32[]{:S(2)}, u32[]{:S(2)}) collective-permute-start(bf16[48,5376]{1,0:T(8,128)(2,1)} %broadcast_select_fusion.2), channel_id=1, source_target_pairs={{16,0},{17,1},{18,2},{19,3},{20,4},{21,5},{22,6},{23,7},{24,8},{25... | collective-permute-start | bytes 1548296 | tf_op jit(solution)/shard_map/while/body/eval_jaxpr/ppermute | solution.py:16
  174.1 1.8 copy-start
  179.4 11.3 %collective-permute-start = (bf16[48,5376]{1,0:T(8,128)(2,1)}, bf16[48,5376]{1,0:T(8,128)(2,1)}, u32[]{:S(2)}, u32[]{:S(2)}) collective-permute-start(bf16[48,5376]{1,0:T(8,128)(2,1)} %broadcast_select_fusion.2), channel_id=1, source_target_pairs={{16,0},{17,1},{18,2},{19,3},{20,4},{21,5},{22,6},{23,7},{24,8},{25... | collective-permute-start | bytes 1548296 | tf_op jit(solution)/shard_map/while/body/eval_jaxpr/ppermute | solution.py:16
  193.8 1.8 copy-start
  201.4 1.8 copy-start.2
  204.5 5.3 %collective-permute-start.1 = (f32[688128]{0:T(1024)}, f32[688128]{0:T(1024)S(1)}, u32[]{:S(2)}, u32[]{:S(2)}) collective-permute-start(f32[688128]{0:T(1024)} %constant_dynamic-update-slice_fusion), channel_id=1, source_target_pairs={{0,1},{1,0},{2,3},{3,2},{4,5},{5,4},{6,7},{7,6},{8,9},{9,8},{10,11... | collective-permute-start | bytes 8257544 | tf_op jit(solution)/shard_map/ppermute | solution.py:93
  211.9 61.8 %collective-permute-start.2 = (f32[688128]{0:T(1024)S(1)}, f32[688128]{0:T(1024)S(1)}, u32[]{:S(2)}, u32[]{:S(2)}) collective-permute-start(f32[688128]{0:T(1024)S(1)} %add.125), channel_id=1, source_target_pairs={{0,2},{1,3},{2,0},{3,1},{4,6},{5,7},{6,4},{7,5},{8,10},{9,11},{10,... | collective-permute-start | bytes 8257544 | tf_op jit(solution)/shard_map/ppermute | solution.py:93
  273.9 65.2 %collective-permute-start.3 = (f32[688128]{0:T(1024)S(1)}, f32[688128]{0:T(1024)}, u32[]{:S(2)}, u32[]{:S(2)}) collective-permute-start(f32[688128]{0:T(1024)S(1)} %add.126), channel_id=1, source_target_pairs={{0,4},{1,5},{2,6},{3,7},{4,0},{5,1},{6,2},{7,3},{8,12},{9,13},{10,... | collective-permute-start | bytes 8257544 | tf_op jit(solution)/shard_map/ppermute | solution.py:93
  274.7 68.1 %all-to-all-start.2 = ((f32[16,1,5376]{2,1,0:T(1,128)}), f32[16,1,5376]{2,1,0:T(1,128)S(1)}, u32[]{:S(2)}, u32[]{:S(2)}) async-start(f32[16,1,5376]{2,1,0:T(1,128)} %bitcast.9), calls=%async_computation.2 | async-start | bytes 688128 | tf_op jit(solution)/shard_map/all_to_all | solution.py:100
  279.6 68.7 %copy-start.5 = (s32[1,8]{1,0:T(1,128)S(1)}, s32[1,8]{1,0:T(1,128)}, u32[]{:S(2)}) copy-start(s32[1,8]{1,0:T(1,128)} %param.19) | copy-start | bytes 100
  279.6 69.2 %copy-start.6 = (s32[1,16]{1,0:T(1,128)S(1)}, s32[1,16]{1,0:T(1,128)}, u32[]{:S(2)}) copy-start(s32[1,16]{1,0:T(1,128)} %param.20) | copy-start | bytes 196
  342.7 155.4 %collective-permute-start.4 = (f32[688128]{0:T(1024)}, f32[688128]{0:T(1024)}, u32[]{:S(2)}, u32[]{:S(2)}) collective-permute-start(f32[688128]{0:T(1024)} %add.127), channel_id=1, source_target_pairs={{0,8},{1,9},{2,10},{3,11},{4,12},{5,13},{6,14},{7,15},{8,0},{9,1},... | collective-permute-start | bytes 8257544 | tf_op jit(solution)/shard_map/ppermute | solution.py:93
  342.8 123.8 %all-to-all-start = ((f32[16,1,5376]{2,1,0:T(1,128)}), f32[16,1,5376]{2,1,0:T(1,128)S(1)}, u32[]{:S(2)}, u32[]{:S(2)}) async-start(f32[16,1,5376]{2,1,0:T(1,128)} %bitcast.5), calls=%async_computation | async-start | bytes 688128 | tf_op jit(solution)/shard_map/all_to_all | solution.py:99
  466.7 16.4 %all-to-all-start.3 = ((f32[16,1,5376]{2,1,0:T(1,128)}), f32[16,1,5376]{2,1,0:T(1,128)S(1)}, u32[]{:S(2)}, u32[]{:S(2)}) async-start(f32[16,1,5376]{2,1,0:T(1,128)} %copy.19), calls=%async_computation.3 | async-start | bytes 688128 | tf_op jit(solution)/shard_map/all_to_all | solution.py:110
  483.0 14.8 %all-to-all-start.1 = ((f32[16,1,5376]{2,1,0:T(1,128)}), f32[16,1,5376]{2,1,0:T(1,128)S(1)}, u32[]{:S(2)}, u32[]{:S(2)}) async-start(f32[16,1,5376]{2,1,0:T(1,128)} %copy.17), calls=%async_computation.1 | async-start | bytes 688128 | tf_op jit(solution)/shard_map/all_to_all | solution.py:109
  (8 other events, 8.9 us)
